TPU v7x, 128 devices: a whole 4x4x4 slice. The times are simulated.
128 devices in a mesh: south: 16 (over z, y), east: 4 (over x), down: 2 (over core).
Axes of the slice: x: 4, y: 4, z: 4, core: 2. Of those that a mesh axis runs over, the one named last changes fastest.
Arguments:
- initial_scalar_state: float32 [64, 128, 256, 128], P('south', 'east', 'down'), may hold values from 0.2 to 1.8
- scaled_wind_second: float32 [64, 128, 256, 128], P('south', 'east', 'down'), may hold values from -0.3 to 0.3
- scaled_wind_first: float32 [64, 128, 256, 128], P('south', 'east', 'down'), may hold values from -0.3 to 0.3
- scaled_wind_third: float32 [64, 128, 256, 128], P('south', 'east', 'down'), may hold values from -0.3 to 0.3
Outputs:
- temperature_end: float32 [64, 128, 256, 128], P('south', 'east', 'down')
All inputs are finite; a program needn't handle non-finite values.
Results may differ from a plain program's by a relative error of at most 0.00002.
Values sent between devices are 32-bit elements; how exact they have to be, the bound alone decides.
A program may use at most 448 MiB of HBM per device.

v0:
```python
import jax
import jax.numpy as jnp
from jax import lax
from jax.sharding import PartitionSpec as P

STEPS = 4


def padded(array, sides, width):
    edges = {}
    for axis, dim in sides:
        size, length = (lax.axis_size(axis), array.shape[dim])
        up = [(i, (i + 1) % size) for i in range(size)]
        last = lax.slice_in_dim(array, length - width, length, axis=dim)
        leading = lax.slice_in_dim(array, 0, width, axis=dim)
        edges[dim] = (
            lax.ppermute(last, axis, up),
            lax.ppermute(leading, axis, [(b, a) for a, b in up]),
        )
    done = []
    for _, dim in sides:
        low, high = edges[dim]
        around = [(width, width) if d in done else (0, 0) for d in range(array.ndim)]
        array = jnp.concatenate([jnp.pad(low, around), array, jnp.pad(high, around)], axis=dim)
        done.append(dim)
    return array


def strip_edges(values, dims):
    for dim in dims:
        values = lax.slice_in_dim(values, 1, values.shape[dim] - 1, axis=dim)
    return values


def neighbour(values, dim, start, dims):
    others = [other for other in dims if other != dim]
    values = strip_edges(values, others)
    return lax.slice_in_dim(values, start, start + values.shape[dim] - 2, axis=dim)


def update_lone_timestep(
    padded_with_margin, scaled_wind_second, scaled_wind_first, scaled_wind_third
):
    middle = strip_edges(padded_with_margin, (0, 1, 2))
    lower = [neighbour(padded_with_margin, dim, 0, (0, 1, 2)) for dim in (0, 1, 2)]
    upper = [neighbour(padded_with_margin, dim, 2, (0, 1, 2)) for dim in (0, 1, 2)]
    slopes = [above - below for above, below in zip(upper, lower)]
    smooth_rate = 0.05
    spread = lower[0] + upper[0] + lower[1] + upper[1] + lower[2] + upper[2] - 6.0 * middle
    return (
        middle
        - scaled_wind_second * slopes[0]
        - scaled_wind_first * slopes[1]
        - scaled_wind_third * slopes[2]
        + smooth_rate * spread
    )


def on_device(initial_scalar_state, scaled_wind_second, scaled_wind_first, scaled_wind_third):
    for step in range(STEPS):
        padded_with_margin = padded(
            initial_scalar_state, (("south", 0), ("east", 1), ("down", 2)), 1
        )
        initial_scalar_state = update_lone_timestep(
            padded_with_margin, scaled_wind_second, scaled_wind_first, scaled_wind_third
        )
    return initial_scalar_state


def solution(mesh):
    placed = (
        P("south", "east", "down", None),
        P("south", "east", "down", None),
        P("south", "east", "down", None),
        P("south", "east", "down", None),
    )
    return jax.shard_map(
        on_device,
        mesh=mesh,
        in_specs=placed,
        out_specs=P("south", "east", "down", None),
        check_vma=False,
    )
```

profile of v0, /device:TPU:0, one launch (start us, length us, event | category | flops | bytes accessed | tf_op | source)
XLA Modules:
  0.0 342.3 jit_solution(2043721420011428729)
XLA Ops:
  0.0 2.6 fusion.19
  4.4 5.0 %collective-permute-start = (f32[1,32,128,128]{3,2,1,0:T(8,128)S(1)}, f32[1,32,128,128]{3,2,1,0:T(8,128)S(1)}, u32[]{:S(2)}, u32[]{:S(2)}) collective-permute-start(f32[1,32,128,128]{3,2,1,0:T(8,128)S(1)} %get-tuple-element.27), channel_id=1, source_target_pairs={{8,0},{16,8},{24,16},{32,24},{40,32},{48,40},{56,48},{64,56},{72,6... | collective-permute-start | bytes 6291464 | tf_op jit(solution)/shard_map/ppermute | solution.py:18
  9.4 2.8 collective-permute-start.2
  12.5 5.1 %collective-permute-done.2 = f32[4,1,128,128]{3,2,1,0:T(8,128)S(1)} collective-permute-done((f32[4,1,128,128]{3,2,1,0:T(8,128)S(1)}, f32[4,1,128,128]{3,2,1,0:T(8,128)S(1)}, u32[]{:S(2)}, u32[]{:S(2)}) %collective-permute-start.2) | collective-permute-done | bytes 262176 | tf_op jit(solution)/shard_map/ppermute | solution.py:18
  17.6 3.4 collective-permute-done.3
  21.0 34.0 %collective-permute-done.1 = f32[1,32,128,128]{3,2,1,0:T(8,128)S(1)} collective-permute-done((f32[1,32,128,128]{3,2,1,0:T(8,128)S(1)}, f32[1,32,128,128]{3,2,1,0:T(8,128)S(1)}, u32[]{:S(2)}, u32[]{:S(2)}) %collective-permute-start.1) | collective-permute-done | bytes 2097184 | tf_op jit(solution)/shard_map/ppermute | solution.py:17
  56.4 4.0 %constant_dynamic-update-slice_fusion.1 = f32[6,32,128,128]{3,2,1,0:T(8,128)} fusion(f32[6,32,128,128]{3,2,1,0:T(8,128)} %constant_dynamic-update-slice_fusion.2, f32[4,32,128,128]{3,2,1,0:T(8,128)S(1)} %copy-done), kind=kLoop, calls=%fused_computation.79 | loop fusion | bytes 16777216
  61.9 30.5 %multiply_add_fusion.3 = f32[4,32,128,128]{3,2,1,0:T(8,128)} fusion(f32[4,32,128,128]{3,2,1,0:T(8,128)} %param.4, f32[4,32,128,128]{3,2,1,0:T(8,128)} %param.7, f32[4,32,1,128]{3,2,1,0:T(1,128)S(1)} %collective-permute-done.4, f32[6,1,128,128]{3,2,1,0:T(8,128)S(1)} %pad.50, f32[6,32,128,128]{3,2,1,0:T(8,128)} %constant_dynamic-update-slice_fusion, ...), kind=kLoop, calls=%fused_computation.77 | loop fusion | flops 71303168 | bytes 59637760 | tf_op jit(solution)/shard_map/add | solution.py:51
  92.5 2.5 fusion.16
  94.9 1.8 collective-permute-start.6
  98.1 2.8 collective-permute-start.8
  102.3 3.0 collective-permute-done.8
  105.4 3.4 collective-permute-done.9
  108.8 33.0 %collective-permute-done.6 = f32[1,32,128,128]{3,2,1,0:T(8,128)S(1)} collective-permute-done((f32[1,32,128,128]{3,2,1,0:T(8,128)S(1)}, f32[1,32,128,128]{3,2,1,0:T(8,128)S(1)}, u32[]{:S(2)}, u32[]{:S(2)}) %collective-permute-start.6) | collective-permute-done | bytes 2097184 | tf_op jit(solution)/shard_map/ppermute | solution.py:18
  141.8 4.6 %collective-permute-done.7 = f32[1,32,128,128]{3,2,1,0:T(8,128)} collective-permute-done((f32[1,32,128,128]{3,2,1,0:T(8,128)S(1)}, f32[1,32,128,128]{3,2,1,0:T(8,128)}, u32[]{:S(2)}, u32[]{:S(2)}) %collective-permute-start.7) | collective-permute-done | bytes 2097184 | tf_op jit(solution)/shard_map/ppermute | solution.py:17
  146.4 31.2 %multiply_add_fusion.2 = f32[4,32,128,128]{3,2,1,0:T(8,128)} fusion(f32[4,32,128,128]{3,2,1,0:T(8,128)} %multiply_add_fusion.3, f32[4,32,128,128]{3,2,1,0:T(8,128)} %param.7, f32[4,32,1,128]{3,2,1,0:T(1,128)S(1)} %collective-permute-done.10, f32[6,1,128,128]{3,2,1,0:T(8,128)S(1)} %pad.54, f32[1,32,128,128]{3,2,1,0:T(8,128)S(1)} %collective-permute-done.6, ...), kind=kLoop, calls=%fused_computation.76 | loop fusion | flops 88080384 | bytes 47054848 | tf_op jit(solution)/shard_map/add | solution.py:51
  177.6 2.5 fusion.13
  180.3 1.8 collective-permute-start.13
  183.3 2.8 collective-permute-start.14
  187.5 2.5 collective-permute-done.14
  190.0 3.7 %collective-permute-done.15 = f32[4,1,128,128]{3,2,1,0:T(8,128)S(1)} collective-permute-done((f32[4,1,128,128]{3,2,1,0:T(8,128)S(1)}, f32[4,1,128,128]{3,2,1,0:T(8,128)S(1)}, u32[]{:S(2)}, u32[]{:S(2)}) %collective-permute-start.15) | collective-permute-done | bytes 262176 | tf_op jit(solution)/shard_map/ppermute | solution.py:17
  193.7 31.8 %collective-permute-done.12 = f32[1,32,128,128]{3,2,1,0:T(8,128)S(1)} collective-permute-done((f32[1,32,128,128]{3,2,1,0:T(8,128)S(1)}, f32[1,32,128,128]{3,2,1,0:T(8,128)S(1)}, u32[]{:S(2)}, u32[]{:S(2)}) %collective-permute-start.12) | collective-permute-done | bytes 2097184 | tf_op jit(solution)/shard_map/ppermute | solution.py:18
  225.5 3.6 %collective-permute-done.13 = f32[1,32,128,128]{3,2,1,0:T(8,128)} collective-permute-done((f32[1,32,128,128]{3,2,1,0:T(8,128)S(1)}, f32[1,32,128,128]{3,2,1,0:T(8,128)}, u32[]{:S(2)}, u32[]{:S(2)}) %collective-permute-start.13) | collective-permute-done | bytes 2097184 | tf_op jit(solution)/shard_map/ppermute | solution.py:17
  229.1 31.2 %multiply_add_fusion.1 = f32[4,32,128,128]{3,2,1,0:T(8,128)} fusion(f32[4,32,128,128]{3,2,1,0:T(8,128)} %multiply_add_fusion.2, f32[4,32,128,128]{3,2,1,0:T(8,128)} %param.7, f32[4,32,1,128]{3,2,1,0:T(1,128)S(1)} %collective-permute-done.16, f32[6,1,128,128]{3,2,1,0:T(8,128)S(1)} %pad.58, f32[1,32,128,128]{3,2,1,0:T(8,128)S(1)} %collective-permute-done.12, ...), kind=kLoop, calls=%fused_computation.75 | loop fusion | flops 88080384 | bytes 47054848 | tf_op jit(solution)/shard_map/add | solution.py:51
  260.3 2.5 fusion.10
  263.1 1.8 collective-permute-start.19
  266.0 2.8 collective-permute-start.20
  270.2 2.5 collective-permute-done.20
  272.8 3.7 %collective-permute-done.21 = f32[4,1,128,128]{3,2,1,0:T(8,128)S(1)} collective-permute-done((f32[4,1,128,128]{3,2,1,0:T(8,128)S(1)}, f32[4,1,128,128]{3,2,1,0:T(8,128)S(1)}, u32[]{:S(2)}, u32[]{:S(2)}) %collective-permute-start.21) | collective-permute-done | bytes 262176 | tf_op jit(solution)/shard_map/ppermute | solution.py:17
  276.5 31.0 %collective-permute-done.18 = f32[1,32,128,128]{3,2,1,0:T(8,128)S(1)} collective-permute-done((f32[1,32,128,128]{3,2,1,0:T(8,128)S(1)}, f32[1,32,128,128]{3,2,1,0:T(8,128)S(1)}, u32[]{:S(2)}, u32[]{:S(2)}) %collective-permute-start.18) | collective-permute-done | bytes 2097184 | tf_op jit(solution)/shard_map/ppermute | solution.py:18
  307.4 3.6 %collective-permute-done.19 = f32[1,32,128,128]{3,2,1,0:T(8,128)} collective-permute-done((f32[1,32,128,128]{3,2,1,0:T(8,128)S(1)}, f32[1,32,128,128]{3,2,1,0:T(8,128)}, u32[]{:S(2)}, u32[]{:S(2)}) %collective-permute-start.19) | collective-permute-done | bytes 2097184 | tf_op jit(solution)/shard_map/ppermute | solution.py:17
  311.0 31.1 %multiply_add_fusion = f32[4,32,128,128]{3,2,1,0:T(8,128)} fusion(f32[4,32,128,128]{3,2,1,0:T(8,128)} %multiply_add_fusion.1, f32[4,32,128,128]{3,2,1,0:T(8,128)} %param.7, f32[4,32,1,128]{3,2,1,0:T(1,128)S(1)} %collective-permute-done.22, f32[6,1,128,128]{3,2,1,0:T(8,128)S(1)} %pad.62, f32[1,32,128,128]{3,2,1,0:T(8,128)S(1)} %collective-permute-done.18, ...), kind=kLoop, calls=%fused_computation.74 | loop fusion | flops 88080384 | bytes 47054848 | tf_op jit(solution)/shard_map/add | solution.py:51
  (45 shorter events, 13.4 us)
Async XLA Ops:
  0.0 9.4 %copy-start = (f32[4,32,128,128]{3,2,1,0:T(8,128)S(1)}, f32[4,32,128,128]{3,2,1,0:T(8,128)}, u32[]{:S(2)}) copy-start(f32[4,32,128,128]{3,2,1,0:T(8,128)} %param.4) | copy-start | bytes 25165828
  2.6 52.3 %collective-permute-start.1 = (f32[1,32,128,128]{3,2,1,0:T(8,128)S(1)}, f32[1,32,128,128]{3,2,1,0:T(8,128)S(1)}, u32[]{:S(2)}, u32[]{:S(2)}) collective-permute-start(f32[1,32,128,128]{3,2,1,0:T(8,128)S(1)} %get-tuple-element.28), channel_id=1, source_target_pairs={{0,8},{8,16},{16,24},{24,32},{32,40},{40,48},{48,56},{56,64},{64,7... | collective-permute-start | bytes 6291464 | tf_op jit(solution)/shard_map/ppermute | solution.py:17
  4.4 56.0 %collective-permute-start = (f32[1,32,128,128]{3,2,1,0:T(8,128)S(1)}, f32[1,32,128,128]{3,2,1,0:T(8,128)S(1)}, u32[]{:S(2)}, u32[]{:S(2)}) collective-permute-start(f32[1,32,128,128]{3,2,1,0:T(8,128)S(1)} %get-tuple-element.27), channel_id=1, source_target_pairs={{8,0},{16,8},{24,16},{32,24},{40,32},{48,40},{56,48},{64,56},{72,6... | collective-permute-start | bytes 6291464 | tf_op jit(solution)/shard_map/ppermute | solution.py:18
  9.4 8.1 %collective-permute-start.2 = (f32[4,1,128,128]{3,2,1,0:T(8,128)S(1)}, f32[4,1,128,128]{3,2,1,0:T(8,128)S(1)}, u32[]{:S(2)}, u32[]{:S(2)}) collective-permute-start(f32[4,1,128,128]{3,2,1,0:T(8,128)S(1)} %get-tuple-element.26), channel_id=1, source_target_pairs={{2,0},{4,2},{6,4},{0,6},{3,1},{5,3},{7,5},{1,7},{10,8},{12,10},{14... | collective-permute-start | bytes 786440 | tf_op jit(solution)/shard_map/ppermute | solution.py:18
  12.3 8.7 %collective-permute-start.3 = (f32[4,1,128,128]{3,2,1,0:T(8,128)S(1)}, f32[4,1,128,128]{3,2,1,0:T(8,128)S(1)}, u32[]{:S(2)}, u32[]{:S(2)}) collective-permute-start(f32[4,1,128,128]{3,2,1,0:T(8,128)S(1)} %get-tuple-element.25), channel_id=1, source_target_pairs={{0,2},{2,4},{4,6},{6,0},{1,3},{3,5},{5,7},{7,1},{8,10},{10,12},{12... | collective-permute-start | bytes 786440 | tf_op jit(solution)/shard_map/ppermute | solution.py:17
  12.4 49.6 %collective-permute-start.4 = (f32[4,32,1,128]{3,2,1,0:T(1,128)S(1)}, f32[4,32,1,128]{3,2,1,0:T(1,128)S(1)}, u32[]{:S(2)}, u32[]{:S(2)}) collective-permute-start(f32[4,32,1,128]{3,2,1,0:T(1,128)S(1)} %get-tuple-element.24), channel_id=1, source_target_pairs={{1,0},{0,1},{3,2},{2,3},{5,4},{4,5},{7,6},{6,7},{9,8},{8,9},{11,10... | collective-permute-start | bytes 196616 | tf_op jit(solution)/shard_map/ppermute | solution.py:18
  17.6 44.4 %collective-permute-start.5 = (f32[4,32,1,128]{3,2,1,0:T(1,128)S(1)}, f32[4,32,1,128]{3,2,1,0:T(1,128)S(1)}, u32[]{:S(2)}, u32[]{:S(2)}) collective-permute-start(f32[4,32,1,128]{3,2,1,0:T(1,128)S(1)} %get-tuple-element.23), channel_id=1, source_target_pairs={{0,1},{1,0},{2,3},{3,2},{4,5},{5,4},{6,7},{7,6},{8,9},{9,8},{10,11... | collective-permute-start | bytes 196616 | tf_op jit(solution)/shard_map/ppermute | solution.py:17
  94.9 46.9 %collective-permute-start.6 = (f32[1,32,128,128]{3,2,1,0:T(8,128)S(1)}, f32[1,32,128,128]{3,2,1,0:T(8,128)S(1)}, u32[]{:S(2)}, u32[]{:S(2)}) collective-permute-start(f32[1,32,128,128]{3,2,1,0:T(8,128)S(1)} %get-tuple-element.22), channel_id=1, source_target_pairs={{8,0},{16,8},{24,16},{32,24},{40,32},{48,40},{56,48},{64,56},{72,6... | collective-permute-start | bytes 6291464 | tf_op jit(solution)/shard_map/ppermute | solution.py:18
  96.8 49.7 %collective-permute-start.7 = (f32[1,32,128,128]{3,2,1,0:T(8,128)S(1)}, f32[1,32,128,128]{3,2,1,0:T(8,128)}, u32[]{:S(2)}, u32[]{:S(2)}) collective-permute-start(f32[1,32,128,128]{3,2,1,0:T(8,128)S(1)} %get-tuple-element.21), channel_id=1, source_target_pairs={{0,8},{8,16},{16,24},{24,32},{32,40},{40,48},{48,56},{56,64},{64,7... | collective-permute-start | bytes 6291464 | tf_op jit(solution)/shard_map/ppermute | solution.py:17
  98.1 7.3 %collective-permute-start.8 = (f32[4,1,128,128]{3,2,1,0:T(8,128)S(1)}, f32[4,1,128,128]{3,2,1,0:T(8,128)S(1)}, u32[]{:S(2)}, u32[]{:S(2)}) collective-permute-start(f32[4,1,128,128]{3,2,1,0:T(8,128)S(1)} %get-tuple-element.20), channel_id=1, source_target_pairs={{2,0},{4,2},{6,4},{0,6},{3,1},{5,3},{7,5},{1,7},{10,8},{12,10},{14... | collective-permute-start | bytes 786440 | tf_op jit(solution)/shard_map/ppermute | solution.py:18
  100.9 7.8 %collective-permute-start.9 = (f32[4,1,128,128]{3,2,1,0:T(8,128)S(1)}, f32[4,1,128,128]{3,2,1,0:T(8,128)S(1)}, u32[]{:S(2)}, u32[]{:S(2)}) collective-permute-start(f32[4,1,128,128]{3,2,1,0:T(8,128)S(1)} %get-tuple-element.19), channel_id=1, source_target_pairs={{0,2},{2,4},{4,6},{6,0},{1,3},{3,5},{5,7},{7,1},{8,10},{10,12},{12... | collective-permute-start | bytes 786440 | tf_op jit(solution)/shard_map/ppermute | solution.py:17
  102.2 6.6 %collective-permute-start.10 = (f32[4,32,1,128]{3,2,1,0:T(1,128)S(1)}, f32[4,32,1,128]{3,2,1,0:T(1,128)S(1)}, u32[]{:S(2)}, u32[]{:S(2)}) collective-permute-start(f32[4,32,1,128]{3,2,1,0:T(1,128)S(1)} %get-tuple-element.18), channel_id=1, source_target_pairs={{1,0},{0,1},{3,2},{2,3},{5,4},{4,5},{7,6},{6,7},{9,8},{8,9},{11,10... | collective-permute-start | bytes 196616 | tf_op jit(solution)/shard_map/ppermute | solution.py:18
  105.4 3.5 %collective-permute-start.11 = (f32[4,32,1,128]{3,2,1,0:T(1,128)S(1)}, f32[4,32,1,128]{3,2,1,0:T(1,128)S(1)}, u32[]{:S(2)}, u32[]{:S(2)}) collective-permute-start(f32[4,32,1,128]{3,2,1,0:T(1,128)S(1)} %get-tuple-element.17), channel_id=1, source_target_pairs={{0,1},{1,0},{2,3},{3,2},{4,5},{5,4},{6,7},{7,6},{8,9},{9,8},{10,11... | collective-permute-start | bytes 196616 | tf_op jit(solution)/shard_map/ppermute | solution.py:17
  180.1 45.4 %collective-permute-start.12 = (f32[1,32,128,128]{3,2,1,0:T(8,128)S(1)}, f32[1,32,128,128]{3,2,1,0:T(8,128)S(1)}, u32[]{:S(2)}, u32[]{:S(2)}) collective-permute-start(f32[1,32,128,128]{3,2,1,0:T(8,128)S(1)} %get-tuple-element.16), channel_id=1, source_target_pairs={{8,0},{16,8},{24,16},{32,24},{40,32},{48,40},{56,48},{64,56},{72,6... | collective-permute-start | bytes 6291464 | tf_op jit(solution)/shard_map/ppermute | solution.py:18
  180.3 48.8 %collective-permute-start.13 = (f32[1,32,128,128]{3,2,1,0:T(8,128)S(1)}, f32[1,32,128,128]{3,2,1,0:T(8,128)}, u32[]{:S(2)}, u32[]{:S(2)}) collective-permute-start(f32[1,32,128,128]{3,2,1,0:T(8,128)S(1)} %get-tuple-element.15), channel_id=1, source_target_pairs={{0,8},{8,16},{16,24},{24,32},{32,40},{40,48},{48,56},{56,64},{64,7... | collective-permute-start | bytes 6291464 | tf_op jit(solution)/shard_map/ppermute | solution.py:17
  183.3 6.7 %collective-permute-start.14 = (f32[4,1,128,128]{3,2,1,0:T(8,128)S(1)}, f32[4,1,128,128]{3,2,1,0:T(8,128)S(1)}, u32[]{:S(2)}, u32[]{:S(2)}) collective-permute-start(f32[4,1,128,128]{3,2,1,0:T(8,128)S(1)} %get-tuple-element.14), channel_id=1, source_target_pairs={{2,0},{4,2},{6,4},{0,6},{3,1},{5,3},{7,5},{1,7},{10,8},{12,10},{14... | collective-permute-start | bytes 786440 | tf_op jit(solution)/shard_map/ppermute | solution.py:18
  186.1 7.6 %collective-permute-start.15 = (f32[4,1,128,128]{3,2,1,0:T(8,128)S(1)}, f32[4,1,128,128]{3,2,1,0:T(8,128)S(1)}, u32[]{:S(2)}, u32[]{:S(2)}) collective-permute-start(f32[4,1,128,128]{3,2,1,0:T(8,128)S(1)} %get-tuple-element.13), channel_id=1, source_target_pairs={{0,2},{2,4},{4,6},{6,0},{1,3},{3,5},{5,7},{7,1},{8,10},{10,12},{12... | collective-permute-start | bytes 786440 | tf_op jit(solution)/shard_map/ppermute | solution.py:17
  187.4 6.3 %collective-permute-start.16 = (f32[4,32,1,128]{3,2,1,0:T(1,128)S(1)}, f32[4,32,1,128]{3,2,1,0:T(1,128)S(1)}, u32[]{:S(2)}, u32[]{:S(2)}) collective-permute-start(f32[4,32,1,128]{3,2,1,0:T(1,128)S(1)} %get-tuple-element.12), channel_id=1, source_target_pairs={{1,0},{0,1},{3,2},{2,3},{5,4},{4,5},{7,6},{6,7},{9,8},{8,9},{11,10... | collective-permute-start | bytes 196616 | tf_op jit(solution)/shard_map/ppermute | solution.py:18
  190.0 3.7 %collective-permute-start.17 = (f32[4,32,1,128]{3,2,1,0:T(1,128)S(1)}, f32[4,32,1,128]{3,2,1,0:T(1,128)S(1)}, u32[]{:S(2)}, u32[]{:S(2)}) collective-permute-start(f32[4,32,1,128]{3,2,1,0:T(1,128)S(1)} %get-tuple-element.11), channel_id=1, source_target_pairs={{0,1},{1,0},{2,3},{3,2},{4,5},{5,4},{6,7},{7,6},{8,9},{9,8},{10,11... | collective-permute-start | bytes 196616 | tf_op jit(solution)/shard_map/ppermute | solution.py:17
  262.8 44.6 %collective-permute-start.18 = (f32[1,32,128,128]{3,2,1,0:T(8,128)S(1)}, f32[1,32,128,128]{3,2,1,0:T(8,128)S(1)}, u32[]{:S(2)}, u32[]{:S(2)}) collective-permute-start(f32[1,32,128,128]{3,2,1,0:T(8,128)S(1)} %get-tuple-element.10), channel_id=1, source_target_pairs={{8,0},{16,8},{24,16},{32,24},{40,32},{48,40},{56,48},{64,56},{72,6... | collective-permute-start | bytes 6291464 | tf_op jit(solution)/shard_map/ppermute | solution.py:18
  263.1 47.9 %collective-permute-start.19 = (f32[1,32,128,128]{3,2,1,0:T(8,128)S(1)}, f32[1,32,128,128]{3,2,1,0:T(8,128)}, u32[]{:S(2)}, u32[]{:S(2)}) collective-permute-start(f32[1,32,128,128]{3,2,1,0:T(8,128)S(1)} %get-tuple-element.9), channel_id=1, source_target_pairs={{0,8},{8,16},{16,24},{24,32},{32,40},{40,48},{48,56},{56,64},{64,7... | collective-permute-start | bytes 6291464 | tf_op jit(solution)/shard_map/ppermute | solution.py:17
  266.0 6.7 %collective-permute-start.20 = (f32[4,1,128,128]{3,2,1,0:T(8,128)S(1)}, f32[4,1,128,128]{3,2,1,0:T(8,128)S(1)}, u32[]{:S(2)}, u32[]{:S(2)}) collective-permute-start(f32[4,1,128,128]{3,2,1,0:T(8,128)S(1)} %get-tuple-element.8), channel_id=1, source_target_pairs={{2,0},{4,2},{6,4},{0,6},{3,1},{5,3},{7,5},{1,7},{10,8},{12,10},{14... | collective-permute-start | bytes 786440 | tf_op jit(solution)/shard_map/ppermute | solution.py:18
  268.8 7.6 %collective-permute-start.21 = (f32[4,1,128,128]{3,2,1,0:T(8,128)S(1)}, f32[4,1,128,128]{3,2,1,0:T(8,128)S(1)}, u32[]{:S(2)}, u32[]{:S(2)}) collective-permute-start(f32[4,1,128,128]{3,2,1,0:T(8,128)S(1)} %get-tuple-element.7), channel_id=1, source_target_pairs={{0,2},{2,4},{4,6},{6,0},{1,3},{3,5},{5,7},{7,1},{8,10},{10,12},{12... | collective-permute-start | bytes 786440 | tf_op jit(solution)/shard_map/ppermute | solution.py:17
  270.1 6.3 %collective-permute-start.22 = (f32[4,32,1,128]{3,2,1,0:T(1,128)S(1)}, f32[4,32,1,128]{3,2,1,0:T(1,128)S(1)}, u32[]{:S(2)}, u32[]{:S(2)}) collective-permute-start(f32[4,32,1,128]{3,2,1,0:T(1,128)S(1)} %get-tuple-element.6), channel_id=1, source_target_pairs={{1,0},{0,1},{3,2},{2,3},{5,4},{4,5},{7,6},{6,7},{9,8},{8,9},{11,10... | collective-permute-start | bytes 196616 | tf_op jit(solution)/shard_map/ppermute | solution.py:18
  272.7 3.7 %collective-permute-start.23 = (f32[4,32,1,128]{3,2,1,0:T(1,128)S(1)}, f32[4,32,1,128]{3,2,1,0:T(1,128)S(1)}, u32[]{:S(2)}, u32[]{:S(2)}) collective-permute-start(f32[4,32,1,128]{3,2,1,0:T(1,128)S(1)} %get-tuple-element.5), channel_id=1, source_target_pairs={{0,1},{1,0},{2,3},{3,2},{4,5},{5,4},{6,7},{7,6},{8,9},{9,8},{10,11... | collective-permute-start | bytes 196616 | tf_op jit(solution)/shard_map/ppermute | solution.py:17
where the time goes:
time: 343 us; the launch traced here: 342 us
  waiting for transfers between devices  169 us (49%)
  other arithmetic  124 us (36%)
  starting transfers between devices  24.7 us (7%)
  local copies, waits for them, and re-layouts  24.5 us (7%)
    add x4, other arithmetic, update_lone_timestep(): middle - scaled_wind_second * slopes[0] - scaled_wind_first * slopes[1]  124 us
    ppermute x12, waiting for transfers between devices, padded(): lax.ppermute(leading, axis, [(b, a) for a, b in up])  109 us
    ppermute x12, waiting for transfers between devices, padded(): lax.ppermute(last, axis, up)  59.8 us
    ppermute x12, starting transfers between devices, padded(): lax.ppermute(leading, axis, [(b, a) for a, b in up])  18.9 us
    slice x11, local copies, waits for them, and re-layouts, padded(): last = lax.slice_in_dim(array, length - width, length, axis=dim)  14.7 us
  transfers between devices with their start and end apart: 24, of which 15 were waited for; matrix products, arithmetic and copies ran while one was open for 4% of the time, Pallas kernels for 0%

commit v1 on v0

v1 whole, which is shorter than its diff:
```python
import functools

import jax
import jax.numpy as jnp
from jax import lax
from jax.experimental import pallas as pl
from jax.experimental.pallas import tpu as pltpu
from jax.sharding import PartitionSpec as P

STEPS = 4
CHUNKS = 8
PAD = 8
MESH = pl.DeviceIdType.MESH
SMOOTH = 0.05


def kernel(
    sizes,
    x_hbm,
    wind_south_hbm,
    wind_east_hbm,
    wind_down_hbm,
    out_hbm,
    state,
    winds,
    load_sem,
    south_send,
    south_recv,
    east_send,
    east_recv,
    down_send,
    down_recv,
    out_sem,
):
    n_south, n_east, n_down = sizes
    planes, rows, depth, _ = x_hbm.shape
    per = rows // CHUNKS
    middle = pl.ds(PAD, depth)
    own_planes = pl.ds(1, planes)

    me_south, me_east, me_down = (lax.axis_index(a) for a in ("south", "east", "down"))
    above = {"south": lax.rem(me_south + 1, n_south)}
    below = {"south": lax.rem(me_south + n_south - 1, n_south)}
    right = {"east": lax.rem(me_east + 1, n_east)}
    left = {"east": lax.rem(me_east + n_east - 1, n_east)}
    partner = {"down": lax.rem(me_down + 1, n_down)}

    loads = []
    for a, ref in enumerate((x_hbm, wind_south_hbm, wind_east_hbm, wind_down_hbm)):
        for p in range(planes):
            target = state.at[0, 1 + p, pl.ds(1, rows), middle] if a == 0 else winds.at[a - 1, p]
            loads.append(pltpu.make_async_copy(ref.at[p], target, load_sem.at[a, p]))
    for load in loads:
        load.start()

    barrier = pltpu.get_barrier_semaphore()
    for neighbour in (above, below, right, left, partner):
        pl.semaphore_signal(barrier, inc=1, device_id=neighbour, device_id_type=MESH)
    pl.semaphore_wait(barrier, 5)

    def remote(src, dst, send, recv, device):
        return pltpu.make_async_remote_copy(
            src_ref=src, dst_ref=dst, send_sem=send, recv_sem=recv, device_id=device, device_id_type=MESH
        )

    def south_copies(n, c):
        slot = n % 2
        here = pl.ds(1 + c * per, per)
        result = []
        for way, (p, halo, device) in enumerate(((planes, 0, above), (1, planes + 1, below))):
            if n == 0:
                src = x_hbm.at[p - 1, pl.ds(c * per, per)]
            else:
                src = state.at[slot, p, here, middle]
            result.append(
                remote(
                    src,
                    state.at[slot, halo, here, middle],
                    south_send.at[way, n, c],
                    south_recv.at[way, n, c],
                    device,
                )
            )
        return result

    def east_copy(n, way):
        slot = n % 2
        r, halo, device = ((rows, 0, right), (1, rows + 1, left))[way]
        src = x_hbm.at[:, r - 1] if n == 0 else state.at[slot, own_planes, r, middle]
        return remote(
            src, state.at[slot, own_planes, halo, middle], east_send.at[way, n], east_recv.at[way, n], device
        )

    def down_copies(n, c):
        slot = n % 2
        here = pl.ds(1 + c * per, per)
        result = []
        for way, (k, halo) in enumerate(((depth - PAD, 0), (0, depth + PAD))):
            if n == 0:
                src = x_hbm.at[:, pl.ds(c * per, per), pl.ds(k, PAD)]
            else:
                src = state.at[slot, own_planes, here, pl.ds(PAD + k, PAD)]
            result.append(
                remote(
                    src,
                    state.at[slot, own_planes, here, pl.ds(halo, PAD)],
                    down_send.at[way, n, c],
                    down_recv.at[way, n, c],
                    partner,
                )
            )
        return result

    def out_copy(c):
        return pltpu.make_async_copy(
            state.at[STEPS % 2, own_planes, pl.ds(1 + c * per, per), middle],
            out_hbm.at[:, pl.ds(c * per, per)],
            out_sem.at[c],
        )

    def compute(n, c, which):
        now, later = n % 2, (n + 1) % 2

        def row(i, carry):
            r = c * per + i
            q = r + 1
            for p in which:
                center = state[now, p, q, middle, :]
                low0 = state[now, p - 1, q, middle, :]
                high0 = state[now, p + 1, q, middle, :]
                low1 = state[now, p, q - 1, middle, :]
                high1 = state[now, p, q + 1, middle, :]
                low2 = state[now, p, q, pl.ds(PAD - 1, depth), :]
                high2 = state[now, p, q, pl.ds(PAD + 1, depth), :]
                spread = low0 + high0 + low1 + high1 + low2 + high2 - 6.0 * center
                state[later, p, q, middle, :] = (
                    center
                    - winds[0, p - 1, r] * (high0 - low0)
                    - winds[1, p - 1, r] * (high1 - low1)
                    - winds[2, p - 1, r] * (high2 - low2)
                    + SMOOTH * spread
                )
            return carry

        lax.fori_loop(0, per, row, 0)

    def start_all(copies):
        for copy in copies:
            copy.start()

    start_all(south_copies(0, 0))
    start_all((east_copy(0, 0), east_copy(0, 1)))

    def first_sends(c, carry):
        start_all(down_copies(0, c))

        @pl.when(c > 0)
        def _():
            start_all(south_copies(0, c))

        return carry

    lax.fori_loop(0, CHUNKS, first_sends, 0)

    for load in loads:
        load.wait()

    edges = (1, planes)
    inner = tuple(range(2, planes))

    for n in range(STEPS):
        for way in (0, 1):
            east_copy(n, way).wait_recv()
            if n > 0:
                east_copy(n - 1, way).wait_send()

        def chunk(c, carry, n=n):
            for copy in down_copies(n, c):
                copy.wait_recv()
            if n > 0:
                for copy in south_copies(n - 1, c) + down_copies(n - 1, c):
                    copy.wait_send()
            if n == STEPS - 1:
                compute(n, c, inner)
            for copy in south_copies(n, c):
                copy.wait_recv()
            compute(n, c, edges)
            if n == STEPS - 1:
                out_copy(c).start()
            else:
                compute(n, c, inner)
                start_all(south_copies(n + 1, c))
                start_all(down_copies(n + 1, c))

                @pl.when(c == 0)
                def _():
                    east_copy(n + 1, 1).start()

                @pl.when(c == CHUNKS - 1)
                def _():
                    east_copy(n + 1, 0).start()

            return carry

        lax.fori_loop(0, CHUNKS, chunk, 0)

    def finish(c, carry):
        for copy in south_copies(STEPS - 1, c) + down_copies(STEPS - 1, c):
            copy.wait_send()
        out_copy(c).wait()
        return carry

    lax.fori_loop(0, CHUNKS, finish, 0)
    for way in (0, 1):
        east_copy(STEPS - 1, way).wait_send()


def solution(mesh):
    sizes = tuple(mesh.shape[a] for a in ("south", "east", "down"))
    spec = P("south", "east", "down", None)

    def on_device(x, wind_south, wind_east, wind_down):
        planes, rows, depth, levels = x.shape
        dma = pltpu.SemaphoreType.DMA
        return pl.pallas_call(
            functools.partial(kernel, sizes),
            out_shape=jax.ShapeDtypeStruct(x.shape, x.dtype),
            in_specs=[pl.BlockSpec(memory_space=pl.ANY)] * 4,
            out_specs=pl.BlockSpec(memory_space=pl.ANY),
            scratch_shapes=[
                pltpu.VMEM((2, planes + 2, rows + 2, depth + 2 * PAD, levels), x.dtype),
                pltpu.VMEM((3, planes, rows, depth, levels), x.dtype),
                dma((4, planes)),
                dma((2, STEPS, CHUNKS)),
                dma((2, STEPS, CHUNKS)),
                dma((2, STEPS)),
                dma((2, STEPS)),
                dma((2, STEPS, CHUNKS)),
                dma((2, STEPS, CHUNKS)),
                dma((CHUNKS,)),
            ],
            compiler_params=pltpu.CompilerParams(
                collective_id=0, has_side_effects=True, vmem_limit_bytes=60 * 1024 * 1024
            ),
            name="advect",
        )(x, wind_south, wind_east, wind_down)

    return jax.shard_map(on_device, mesh=mesh, in_specs=(spec,) * 4, out_specs=spec, check_vma=False)
```

time: 343 us -> 202 us (0.59)
  Pallas kernels: 0 us -> 194 us
  waiting for transfers between devices: 169 us -> 0 us
  other arithmetic: 124 us -> 0 us
  starting transfers between devices: 24.7 us -> 0 us
  local copies, waits for them, and re-layouts: 24.5 us -> 7.89 us
    pallas_call x0 -> x1, Pallas kernels: none -> 194 us  [on_device(): pl.pallas_call(functools.partial(kernel, sizes), out_shape=jax.ShapeDtype...]
    ppermute x24 -> x0, waiting for transfers between devices: 169 us -> none  [the longest x12 109 us: padded(): lax.ppermute(leading, axis, [(b, a) for a, b in up])]
    add x4 -> x0, other arithmetic: 124 us -> none  [update_lone_timestep(): middle - scaled_wind_second * slopes[0] - scaled_wind_first * slopes[1]]
    ppermute x24 -> x0, starting transfers between devices: 24.7 us -> none  [the longest x12 18.9 us: padded(): lax.ppermute(leading, axis, [(b, a) for a, b in up])]
    slice x12 -> x0, local copies, waits for them, and re-layouts: 17.3 us -> none  [the longest x11 14.7 us: padded(): last = lax.slice_in_dim(array, length - width, length, axis=dim)]
    unnamed x4 -> x1, local copies, waits for them, and re-layouts: 5.47 us -> 7.89 us
  transfers between devices with their start and end apart: 24 -> 0, of which waited for: 15 -> 0; matrix products, arithmetic and copies ran while one was open for 4% -> 0% of each run, Pallas kernels for 0% -> 0%
where the time goes in v1:
time: 202 us
  Pallas kernels  194 us (96%)
  local copies, waits for them, and re-layouts  7.89 us (4%)
    pallas_call x1, Pallas kernels, on_device(): pl.pallas_call(functools.partial(kernel, sizes), out_shape=jax.ShapeDtype...  194 us
    unnamed x1, local copies, waits for them, and re-layouts  7.89 us

profile of v1, /device:TPU:0, one launch (start us, length us, event | category | flops | bytes accessed | tf_op | source)
XLA Modules:
  0.0 201.7 jit_solution(9048699055653650811)
XLA Ops:
  0.0 193.8 %advect.1 = f32[4,32,128,128]{3,2,1,0:T(8,128)} custom-call(f32[4,32,128,128]{3,2,1,0:T(8,128)} %x_hbm.1, f32[4,32,128,128]{3,2,1,0:T(8,128)} %wind_south_hbm.1, f32[4,32,128,128]{3,2,1,0:T(8,128)} %wind_east_hbm.1, f32[4,32,128,128]{3,2,1,0:T(8,128)} %wind_down_hbm.1), custom_call_target="tpu_custom_call" | custom-call | tf_op jit(solution)/shard_map/advect/pallas_call | solution.py:225
  193.8 7.9 %copy.6 = f32[4,32,128,128]{3,2,1,0:T(8,128)} copy(f32[4,32,128,128]{3,2,1,0:T(8,128)} %advect.1) | data formatting | bytes 16777216

commit v2 on v1

v2 whole, which is shorter than its diff:
```python
import functools

import jax
from jax import lax
from jax.experimental import pallas as pl
from jax.experimental.pallas import tpu as pltpu
from jax.sharding import PartitionSpec as P

STEPS = 4
PARTS = (14, 14, 2, 2)
PAD = 8
MESH = pl.DeviceIdType.MESH
SMOOTH = 0.05


def kernel(
    sizes,
    parts,
    x_hbm,
    wind_south_hbm,
    wind_east_hbm,
    wind_down_hbm,
    out,
    state,
    winds,
    load_sem,
    south_send,
    south_recv,
    east_send,
    east_recv,
    down_send,
    down_recv,
):
    n_south, n_east, n_down = sizes
    planes, rows, depth, _ = x_hbm.shape
    middle = pl.ds(PAD, depth)
    own_planes = pl.ds(1, planes)

    me_south, me_east, me_down = (lax.axis_index(a) for a in ("south", "east", "down"))
    above = {"south": lax.rem(me_south + 1, n_south)}
    below = {"south": lax.rem(me_south + n_south - 1, n_south)}
    right = {"east": lax.rem(me_east + 1, n_east)}
    left = {"east": lax.rem(me_east + n_east - 1, n_east)}
    partner = {"down": lax.rem(me_down + 1, n_down)}

    barrier = pltpu.get_barrier_semaphore()
    for neighbour in (above, below, right, left, partner):
        pl.semaphore_signal(barrier, inc=1, device_id=neighbour, device_id_type=MESH)
    pl.semaphore_wait(barrier, 5)

    def remote(src, dst, send, recv, device):
        return pltpu.make_async_remote_copy(
            src_ref=src, dst_ref=dst, send_sem=send, recv_sem=recv, device_id=device, device_id_type=MESH
        )

    def south_copies(n, c):
        slot = n % 2
        first, size = parts[c]
        here = pl.ds(1 + first, size)
        result = []
        for way, (p, halo, device) in enumerate(((planes, 0, above), (1, planes + 1, below))):
            if n == 0:
                src = x_hbm.at[p - 1, pl.ds(first, size)]
            else:
                src = state.at[slot, p, here, middle]
            dst = state.at[slot, halo, here, middle]
            result.append(remote(src, dst, south_send.at[way, n, c], south_recv.at[way, n, c], device))
        return result

    def east_copy(n, way):
        slot = n % 2
        r, halo, device = ((rows, 0, right), (1, rows + 1, left))[way]
        src = x_hbm.at[:, r - 1] if n == 0 else state.at[slot, own_planes, r, middle]
        dst = state.at[slot, own_planes, halo, middle]
        return remote(src, dst, east_send.at[way, n], east_recv.at[way, n], device)

    def down_copies(n, c):
        slot = n % 2
        first, size = parts[c]
        here = pl.ds(1 + first, size)
        result = []
        for way, (k, halo) in enumerate(((depth - PAD, 0), (0, depth + PAD))):
            if n == 0:
                src = x_hbm.at[:, pl.ds(first, size), pl.ds(k, PAD)]
            else:
                src = state.at[slot, own_planes, here, pl.ds(PAD + k, PAD)]
            dst = state.at[slot, own_planes, here, pl.ds(halo, PAD)]
            result.append(remote(src, dst, down_send.at[way, n, c], down_recv.at[way, n, c], partner))
        return result

    def compute(n, c, which):
        now, later = n % 2, (n + 1) % 2
        first, size = parts[c]

        def row(r, carry):
            q = r + 1
            for p in which:
                center = state[now, p, q, middle, :]
                low0 = state[now, p - 1, q, middle, :]
                high0 = state[now, p + 1, q, middle, :]
                low1 = state[now, p, q - 1, middle, :]
                high1 = state[now, p, q + 1, middle, :]
                low2 = state[now, p, q, pl.ds(PAD - 1, depth), :]
                high2 = state[now, p, q, pl.ds(PAD + 1, depth), :]
                spread = low0 + high0 + low1 + high1 + low2 + high2 - 6.0 * center
                value = (
                    center
                    - winds[0, p - 1, r] * (high0 - low0)
                    - winds[1, p - 1, r] * (high1 - low1)
                    - winds[2, p - 1, r] * (high2 - low2)
                    + SMOOTH * spread
                )
                if n == STEPS - 1:
                    out[p - 1, r] = value
                else:
                    state[later, p, q, middle, :] = value
            return carry

        lax.fori_loop(first, first + size, row, 0)

    def start_all(copies):
        for copy in copies:
            copy.start()

    count = len(parts)
    for c in range(count):
        start_all(south_copies(0, c))
        if c == 0:
            start_all((east_copy(0, 0), east_copy(0, 1)))
        start_all(down_copies(0, c))

    loads = []
    for a, ref in enumerate((x_hbm, wind_south_hbm, wind_east_hbm, wind_down_hbm)):
        for p in range(planes):
            target = state.at[0, 1 + p, pl.ds(1, rows), middle] if a == 0 else winds.at[a - 1, p]
            loads.append(pltpu.make_async_copy(ref.at[p], target, load_sem.at[a, p]))
    start_all(loads)
    for load in loads:
        load.wait()

    edges = (1, planes)
    inner = tuple(range(2, planes))

    for n in range(STEPS):
        last = n == STEPS - 1
        for way in (0, 1):
            east_copy(n, way).wait_recv()
            if n > 0:
                east_copy(n - 1, way).wait_send()

        for c in range(count):
            for copy in down_copies(n, c):
                copy.wait_recv()
            if n > 0:
                for copy in south_copies(n - 1, c) + down_copies(n - 1, c):
                    copy.wait_send()
            if last:
                compute(n, c, inner)
            for copy in south_copies(n, c):
                copy.wait_recv()
            compute(n, c, edges)
            if not last:
                compute(n, c, inner)
                start_all(south_copies(n + 1, c))
                start_all(down_copies(n + 1, c))
                if c == 0:
                    east_copy(n + 1, 1).start()
                if c == count - 1:
                    east_copy(n + 1, 0).start()

    for c in range(count):
        for copy in south_copies(STEPS - 1, c) + down_copies(STEPS - 1, c):
            copy.wait_send()
    for way in (0, 1):
        east_copy(STEPS - 1, way).wait_send()


def solution(mesh):
    sizes = tuple(mesh.shape[a] for a in ("south", "east", "down"))
    spec = P("south", "east", "down", None)

    def on_device(x, wind_south, wind_east, wind_down):
        planes, rows, depth, levels = x.shape
        parts, first = [], 0
        for share in PARTS:
            parts.append((first, share * rows // sum(PARTS)))
            first += parts[-1][1]
        dma = pltpu.SemaphoreType.DMA
        return pl.pallas_call(
            functools.partial(kernel, sizes, tuple(parts)),
            out_shape=pltpu.VMEM(x.shape, x.dtype),
            in_specs=[pl.BlockSpec(memory_space=pltpu.HBM)] * 4,
            out_specs=pl.BlockSpec(memory_space=pltpu.VMEM),
            scratch_shapes=[
                pltpu.VMEM((2, planes + 2, rows + 2, depth + 2 * PAD, levels), x.dtype),
                pltpu.VMEM((3, planes, rows, depth, levels), x.dtype),
                dma((4, planes)),
                dma((2, STEPS, len(parts))),
                dma((2, STEPS, len(parts))),
                dma((2, STEPS)),
                dma((2, STEPS)),
                dma((2, STEPS, len(parts))),
                dma((2, STEPS, len(parts))),
            ],
            compiler_params=pltpu.CompilerParams(
                collective_id=0, has_side_effects=True, vmem_limit_bytes=54 * 1024 * 1024
            ),
            name="advect",
        )(x, wind_south, wind_east, wind_down)

    return jax.shard_map(on_device, mesh=mesh, in_specs=(spec,) * 4, out_specs=spec, check_vma=False)
```

time: 202 us -> 195 us (0.965)
  local copies, waits for them, and re-layouts: 7.89 us -> 3.4 us
  Pallas kernels: 194 us -> 191 us
    unnamed x1, local copies, waits for them, and re-layouts: 7.89 us -> 3.4 us
    pallas_call x1, Pallas kernels: 194 us -> 191 us  [on_device(): pl.pallas_call(functools.partial(kernel, sizes, tuple(parts)), out_shape=...]
where the time goes in v2:
time: 195 us
  Pallas kernels  191 us (98%)
  local copies, waits for them, and re-layouts  3.4 us (2%)
    pallas_call x1, Pallas kernels, on_device(): pl.pallas_call(functools.partial(kernel, sizes, tuple(parts)), out_shape=...  191 us

profile of v2, /device:TPU:0, one launch (start us, length us, event | category | flops | bytes accessed | tf_op | source)
XLA Modules:
  0.0 194.8 jit_solution(13974826454090427144)
XLA Ops:
  0.0 191.4 %advect.1 = f32[4,32,128,128]{3,2,1,0:T(8,128)S(1)} custom-call(f32[4,32,128,128]{3,2,1,0:T(8,128)} %x_hbm.1, f32[4,32,128,128]{3,2,1,0:T(8,128)} %wind_south_hbm.1, f32[4,32,128,128]{3,2,1,0:T(8,128)} %wind_east_hbm.1, f32[4,32,128,128]{3,2,1,0:T(8,128)} %wind_down_hbm.1), custom_call_target="tpu_custom_call" | custom-call | tf_op jit(solution)/shard_map/advect/pallas_call | solution.py:189
  191.4 3.4 %copy.6 = f32[4,32,128,128]{3,2,1,0:T(8,128)} copy(f32[4,32,128,128]{3,2,1,0:T(8,128)S(1)} %advect.1) | data formatting | bytes 16777216

commit v3 on v2

--- a/solution.py
+++ b/solution.py
@@ -7,7 +7,7 @@
 from jax.sharding import PartitionSpec as P
 
 STEPS = 4
-PARTS = (14, 14, 2, 2)
+PARTS = (2, 14, 14, 2)
 PAD = 8
 MESH = pl.DeviceIdType.MESH
 SMOOTH = 0.05
@@ -43,6 +43,16 @@
     left = {"east": lax.rem(me_east + n_east - 1, n_east)}
     partner = {"down": lax.rem(me_down + 1, n_down)}
 
+    first, size = parts[0]
+    heads = [
+        pltpu.make_async_copy(
+            x_hbm.at[p - 1, pl.ds(first, size)], state.at[0, p, pl.ds(1 + first, size), middle], load_sem.at[i]
+        )
+        for i, p in ((0, planes), (1, 1))
+    ]
+    for head in heads:
+        head.start()
+
     barrier = pltpu.get_barrier_semaphore()
     for neighbour in (above, below, right, left, partner):
         pl.semaphore_signal(barrier, inc=1, device_id=neighbour, device_id_type=MESH)
@@ -59,12 +69,12 @@
         here = pl.ds(1 + first, size)
         result = []
         for way, (p, halo, device) in enumerate(((planes, 0, above), (1, planes + 1, below))):
-            if n == 0:
+            if n == 0 and c > 0:
                 src = x_hbm.at[p - 1, pl.ds(first, size)]
             else:
                 src = state.at[slot, p, here, middle]
             dst = state.at[slot, halo, here, middle]
-            result.append(remote(src, dst, south_send.at[way, n, c], south_recv.at[way, n, c], device))
+            result.append(remote(src, dst, south_send.at[way, slot, c], south_recv.at[way, slot, c], device))
         return result
 
     def east_copy(n, way):
@@ -72,20 +82,19 @@
         r, halo, device = ((rows, 0, right), (1, rows + 1, left))[way]
         src = x_hbm.at[:, r - 1] if n == 0 else state.at[slot, own_planes, r, middle]
         dst = state.at[slot, own_planes, halo, middle]
-        return remote(src, dst, east_send.at[way, n], east_recv.at[way, n], device)
-
-    def down_copies(n, c):
+        return remote(src, dst, east_send.at[way, slot], east_recv.at[way, slot], device)
+
+    def down_copies(n):
         slot = n % 2
-        first, size = parts[c]
-        here = pl.ds(1 + first, size)
+        here = pl.ds(1, rows)
         result = []
         for way, (k, halo) in enumerate(((depth - PAD, 0), (0, depth + PAD))):
             if n == 0:
-                src = x_hbm.at[:, pl.ds(first, size), pl.ds(k, PAD)]
+                src = x_hbm.at[:, :, pl.ds(k, PAD)]
             else:
                 src = state.at[slot, own_planes, here, pl.ds(PAD + k, PAD)]
             dst = state.at[slot, own_planes, here, pl.ds(halo, PAD)]
-            result.append(remote(src, dst, down_send.at[way, n, c], down_recv.at[way, n, c], partner))
+            result.append(remote(src, dst, down_send.at[way, slot], down_recv.at[way, slot], partner))
         return result
 
     def compute(n, c, which):
@@ -123,17 +132,27 @@
             copy.start()
 
     count = len(parts)
+    for head in heads:
+        head.wait()
     for c in range(count):
         start_all(south_copies(0, c))
         if c == 0:
             start_all((east_copy(0, 0), east_copy(0, 1)))
-        start_all(down_copies(0, c))
-
-    loads = []
-    for a, ref in enumerate((x_hbm, wind_south_hbm, wind_east_hbm, wind_down_hbm)):
-        for p in range(planes):
-            target = state.at[0, 1 + p, pl.ds(1, rows), middle] if a == 0 else winds.at[a - 1, p]
-            loads.append(pltpu.make_async_copy(ref.at[p], target, load_sem.at[a, p]))
+            start_all(down_copies(0))
+
+    rest = rows - size
+    loads = [
+        pltpu.make_async_copy(
+            x_hbm.at[:, pl.ds(size, rest)], state.at[0, own_planes, pl.ds(1 + size, rest), middle], load_sem.at[0]
+        ),
+        pltpu.make_async_copy(
+            x_hbm.at[pl.ds(1, planes - 2), pl.ds(0, size)],
+            state.at[0, pl.ds(2, planes - 2), pl.ds(1, size), middle],
+            load_sem.at[4],
+        ),
+    ]
+    for d, ref in enumerate((wind_south_hbm, wind_east_hbm, wind_down_hbm)):
+        loads.append(pltpu.make_async_copy(ref, winds.at[d], load_sem.at[1 + d]))
     start_all(loads)
     for load in loads:
         load.wait()
@@ -143,16 +162,15 @@
 
     for n in range(STEPS):
         last = n == STEPS - 1
-        for way in (0, 1):
-            east_copy(n, way).wait_recv()
+        for copy in [east_copy(n, 0), east_copy(n, 1)] + down_copies(n):
+            copy.wait_recv()
+        if n > 0:
+            for copy in [east_copy(n - 1, 0), east_copy(n - 1, 1)] + down_copies(n - 1):
+                copy.wait_send()
+
+        for c in range(count):
             if n > 0:
-                east_copy(n - 1, way).wait_send()
-
-        for c in range(count):
-            for copy in down_copies(n, c):
-                copy.wait_recv()
-            if n > 0:
-                for copy in south_copies(n - 1, c) + down_copies(n - 1, c):
+                for copy in south_copies(n - 1, c):
                     copy.wait_send()
             if last:
                 compute(n, c, inner)
@@ -162,17 +180,17 @@
             if not last:
                 compute(n, c, inner)
                 start_all(south_copies(n + 1, c))
-                start_all(down_copies(n + 1, c))
                 if c == 0:
                     east_copy(n + 1, 1).start()
                 if c == count - 1:
                     east_copy(n + 1, 0).start()
+                    start_all(down_copies(n + 1))
 
     for c in range(count):
-        for copy in south_copies(STEPS - 1, c) + down_copies(STEPS - 1, c):
+        for copy in south_copies(STEPS - 1, c):
             copy.wait_send()
-    for way in (0, 1):
-        east_copy(STEPS - 1, way).wait_send()
+    for copy in [east_copy(STEPS - 1, 0), east_copy(STEPS - 1, 1)] + down_copies(STEPS - 1):
+        copy.wait_send()
 
 
 def solution(mesh):
@@ -194,13 +212,13 @@
             scratch_shapes=[
                 pltpu.VMEM((2, planes + 2, rows + 2, depth + 2 * PAD, levels), x.dtype),
                 pltpu.VMEM((3, planes, rows, depth, levels), x.dtype),
-                dma((4, planes)),
-                dma((2, STEPS, len(parts))),
-                dma((2, STEPS, len(parts))),
-                dma((2, STEPS)),
-                dma((2, STEPS)),
-                dma((2, STEPS, len(parts))),
-                dma((2, STEPS, len(parts))),
+                dma((5,)),
+                dma((2, 2, len(parts))),
+                dma((2, 2, len(parts))),
+                dma((2, 2)),
+                dma((2, 2)),
+                dma((2, 2)),
+                dma((2, 2)),
             ],
             compiler_params=pltpu.CompilerParams(
                 collective_id=0, has_side_effects=True, vmem_limit_bytes=54 * 1024 * 1024

time: 195 us -> 194 us (level)
  no operation moved by 1% of the time
where the time goes in v3:
time: 194 us
  Pallas kernels  190 us (98%)
  local copies, waits for them, and re-layouts  3.4 us (2%)
    pallas_call x1, Pallas kernels, on_device(): pl.pallas_call(functools.partial(kernel, sizes, tuple(parts)), out_shape=...  190 us

profile of v3, /device:TPU:0, one launch (start us, length us, event | category | flops | bytes accessed | tf_op | source)
XLA Modules:
  0.0 193.6 jit_solution(12990462281422996410)
XLA Ops:
  0.0 190.2 %advect.1 = f32[4,32,128,128]{3,2,1,0:T(8,128)S(1)} custom-call(f32[4,32,128,128]{3,2,1,0:T(8,128)} %x_hbm.1, f32[4,32,128,128]{3,2,1,0:T(8,128)} %wind_south_hbm.1, f32[4,32,128,128]{3,2,1,0:T(8,128)} %wind_east_hbm.1, f32[4,32,128,128]{3,2,1,0:T(8,128)} %wind_down_hbm.1), custom_call_target="tpu_custom_call" | custom-call | tf_op jit(solution)/shard_map/advect/pallas_call | solution.py:207
  190.2 3.4 %copy.6 = f32[4,32,128,128]{3,2,1,0:T(8,128)} copy(f32[4,32,128,128]{3,2,1,0:T(8,128)S(1)} %advect.1) | data formatting | bytes 16777216

commit v4 on v3

--- a/solution.py
+++ b/solution.py
@@ -1,13 +1,20 @@
 import functools
 
 import jax
+import jax.numpy as jnp
 from jax import lax
 from jax.experimental import pallas as pl
 from jax.experimental.pallas import tpu as pltpu
 from jax.sharding import PartitionSpec as P
 
 STEPS = 4
-PARTS = (2, 14, 14, 2)
+PARTS = (
+    ((2, 0), (14, 1), (16, 2)),
+    ((16, 3), (16, 4)),
+    ((16, 0), (16, 2)),
+    ((14, 3), (16, 4), (2, 1)),
+)
+FACE_SEMAPHORES = 6
 PAD = 8
 MESH = pl.DeviceIdType.MESH
 SMOOTH = 0.05
@@ -30,6 +37,7 @@
     east_recv,
     down_send,
     down_recv,
+    told,
 ):
     n_south, n_east, n_down = sizes
     planes, rows, depth, _ = x_hbm.shape
@@ -43,7 +51,7 @@
     left = {"east": lax.rem(me_east + n_east - 1, n_east)}
     partner = {"down": lax.rem(me_down + 1, n_down)}
 
-    first, size = parts[0]
+    first, size, _ = parts[0][0]
     heads = [
         pltpu.make_async_copy(
             x_hbm.at[p - 1, pl.ds(first, size)], state.at[0, p, pl.ds(1 + first, size), middle], load_sem.at[i]
@@ -54,27 +62,38 @@
         head.start()
 
     barrier = pltpu.get_barrier_semaphore()
-    for neighbour in (above, below, right, left, partner):
+    for neighbour in ({**above, "down": 0}, below, {**right, "down": 0}, {**left, "down": 0}):
         pl.semaphore_signal(barrier, inc=1, device_id=neighbour, device_id_type=MESH)
-    pl.semaphore_wait(barrier, 5)
+
+    @pl.when(me_down == 1)
+    def _():
+        pl.semaphore_signal(barrier, inc=1, device_id=partner, device_id_type=MESH)
+
+    pl.semaphore_wait(barrier, jnp.where(me_down == 1, 1, 8))
+
+    @pl.when(me_down == 0)
+    def _():
+        pl.semaphore_signal(told, inc=1, device_id=partner, device_id_type=MESH)
+
 
     def remote(src, dst, send, recv, device):
         return pltpu.make_async_remote_copy(
             src_ref=src, dst_ref=dst, send_sem=send, recv_sem=recv, device_id=device, device_id_type=MESH
         )
 
-    def south_copies(n, c):
+    def south_copies(n, c, ways=(0, 1)):
         slot = n % 2
-        first, size = parts[c]
+        first, size, sem = parts[n][c]
         here = pl.ds(1 + first, size)
         result = []
-        for way, (p, halo, device) in enumerate(((planes, 0, above), (1, planes + 1, below))):
+        for way in ways:
+            p, halo, device = ((planes, 0, above), (1, planes + 1, below))[way]
             if n == 0 and c > 0:
                 src = x_hbm.at[p - 1, pl.ds(first, size)]
             else:
                 src = state.at[slot, p, here, middle]
             dst = state.at[slot, halo, here, middle]
-            result.append(remote(src, dst, south_send.at[way, slot, c], south_recv.at[way, slot, c], device))
+            result.append(remote(src, dst, south_send.at[way, sem], south_recv.at[way, sem], device))
         return result
 
     def east_copy(n, way):
@@ -99,7 +118,7 @@
 
     def compute(n, c, which):
         now, later = n % 2, (n + 1) % 2
-        first, size = parts[c]
+        first, size, _ = parts[n][c]
 
         def row(r, carry):
             q = r + 1
@@ -131,14 +150,19 @@
         for copy in copies:
             copy.start()
 
-    count = len(parts)
     for head in heads:
         head.wait()
-    for c in range(count):
-        start_all(south_copies(0, c))
-        if c == 0:
-            start_all((east_copy(0, 0), east_copy(0, 1)))
-            start_all(down_copies(0))
+    for c in range(len(parts[0])):
+        start_all(south_copies(0, c, (0,)))
+
+    @pl.when(me_down == 1)
+    def _():
+        pl.semaphore_wait(told, 1)
+
+    for c in range(len(parts[0])):
+        start_all(south_copies(0, c, (1,)))
+    start_all((east_copy(0, 0), east_copy(0, 1)))
+    start_all(down_copies(0))
 
     rest = rows - size
     loads = [
@@ -159,6 +183,8 @@
 
     edges = (1, planes)
     inner = tuple(range(2, planes))
+    ready = [list(range(len(step))) for step in parts]
+    sent = [list(range(len(step))) for step in parts]
 
     for n in range(STEPS):
         last = n == STEPS - 1
@@ -168,10 +194,13 @@
             for copy in [east_copy(n - 1, 0), east_copy(n - 1, 1)] + down_copies(n - 1):
                 copy.wait_send()
 
+        count = len(parts[n])
         for c in range(count):
-            if n > 0:
-                for copy in south_copies(n - 1, c):
-                    copy.wait_send()
+            end = parts[n][c][0] + parts[n][c][1]
+            if 0 < n and not last:
+                while sent[n - 1] and parts[n - 1][sent[n - 1][0]][0] < end:
+                    for copy in south_copies(n - 1, sent[n - 1].pop(0)):
+                        copy.wait_send()
             if last:
                 compute(n, c, inner)
             for copy in south_copies(n, c):
@@ -179,16 +208,18 @@
             compute(n, c, edges)
             if not last:
                 compute(n, c, inner)
-                start_all(south_copies(n + 1, c))
+                while ready[n + 1] and sum(parts[n + 1][ready[n + 1][0]][:2]) <= end:
+                    start_all(south_copies(n + 1, ready[n + 1].pop(0)))
                 if c == 0:
                     east_copy(n + 1, 1).start()
                 if c == count - 1:
                     east_copy(n + 1, 0).start()
                     start_all(down_copies(n + 1))
 
-    for c in range(count):
-        for copy in south_copies(STEPS - 1, c):
-            copy.wait_send()
+    for n in range(STEPS):
+        for c in sent[n]:
+            for copy in south_copies(n, c):
+                copy.wait_send()
     for copy in [east_copy(STEPS - 1, 0), east_copy(STEPS - 1, 1)] + down_copies(STEPS - 1):
         copy.wait_send()
 
@@ -199,13 +230,17 @@
 
     def on_device(x, wind_south, wind_east, wind_down):
         planes, rows, depth, levels = x.shape
-        parts, first = [], 0
-        for share in PARTS:
-            parts.append((first, share * rows // sum(PARTS)))
-            first += parts[-1][1]
+        parts = []
+        for step in PARTS:
+            parts.append([])
+            first = 0
+            for share, semaphore in step:
+                size = share * rows // 32
+                parts[-1].append((first, size, semaphore))
+                first += size
         dma = pltpu.SemaphoreType.DMA
         return pl.pallas_call(
-            functools.partial(kernel, sizes, tuple(parts)),
+            functools.partial(kernel, sizes, parts),
             out_shape=pltpu.VMEM(x.shape, x.dtype),
             in_specs=[pl.BlockSpec(memory_space=pltpu.HBM)] * 4,
             out_specs=pl.BlockSpec(memory_space=pltpu.VMEM),
@@ -213,12 +248,13 @@
                 pltpu.VMEM((2, planes + 2, rows + 2, depth + 2 * PAD, levels), x.dtype),
                 pltpu.VMEM((3, planes, rows, depth, levels), x.dtype),
                 dma((5,)),
-                dma((2, 2, len(parts))),
-                dma((2, 2, len(parts))),
-                dma((2, 2)),
-                dma((2, 2)),
-                dma((2, 2)),
-                dma((2, 2)),
+                dma((2, FACE_SEMAPHORES)),
+                dma((2, FACE_SEMAPHORES)),
+                dma((2, 2)),
+                dma((2, 2)),
+                dma((2, 2)),
+                dma((2, 2)),
+                pltpu.SemaphoreType.REGULAR,
             ],
             compiler_params=pltpu.CompilerParams(
                 collective_id=0, has_side_effects=True, vmem_limit_bytes=54 * 1024 * 1024

time: 194 us -> 192 us (0.990)
  no operation moved by 1% of the time
where the time goes in v4:
time: 192 us
  Pallas kernels  189 us (98%)
  local copies, waits for them, and re-layouts  3.4 us (2%)
    pallas_call x1, Pallas kernels, on_device(): pl.pallas_call(functools.partial(kernel, sizes, parts), out_shape=pltpu.V...  189 us

profile of v4, /device:TPU:0, one launch (start us, length us, event | category | flops | bytes accessed | tf_op | source)
XLA Modules:
  0.0 192.3 jit_solution(7489880073999927990)
XLA Ops:
  0.0 188.9 %advect.1 = f32[4,32,128,128]{3,2,1,0:T(8,128)S(1)} custom-call(f32[4,32,128,128]{3,2,1,0:T(8,128)} %x_hbm.1, f32[4,32,128,128]{3,2,1,0:T(8,128)} %wind_south_hbm.1, f32[4,32,128,128]{3,2,1,0:T(8,128)} %wind_east_hbm.1, f32[4,32,128,128]{3,2,1,0:T(8,128)} %wind_down_hbm.1), custom_call_target="tpu_custom_call" | custom-call | tf_op jit(solution)/shard_map/advect/pallas_call | solution.py:242
  188.9 3.4 %copy.6 = f32[4,32,128,128]{3,2,1,0:T(8,128)} copy(f32[4,32,128,128]{3,2,1,0:T(8,128)S(1)} %advect.1) | data formatting | bytes 16777216
